TPU v7x, 256 devices: a whole 4x4x8 slice. The times are simulated.
256 devices in a mesh: dp: 8 (over z_lo, core), ep: 32 (over x, y, z_hi).
Axes of the slice: x: 4, y: 4, z: 8 (z_hi: 2, z_lo: 4; z = z_hi * 4 + z_lo), core: 2. Of those that a mesh axis runs over, the one named last changes fastest.
Arguments:
- tokens: bfloat16 [32768, 7168], P(('dp', 'ep')), may hold values from -6 to 6
- out_grad: bfloat16 [32768, 7168], P(('dp', 'ep')), may hold values from -3 to 3
- expert_ids: int32 [32768, 8], P(('dp', 'ep')), may hold values from 0 to 255, as said below
- route_weights: bfloat16 [32768, 8], P(('dp', 'ep')), may hold values from 0.099609375 to 1
- gate_matrix: bfloat16 [7168, 8192], P('dp', 'ep'), may hold values from -0.0625 to 0.0625
- up_matrix: bfloat16 [7168, 8192], P('dp', 'ep'), may hold values from -0.0625 to 0.0625
- down_matrix: bfloat16 [7168, 8192], P('dp', 'ep'), may hold values from -0.125 to 0.125
Outputs:
- input_gradient: bfloat16 [32768, 7168], P(('dp', 'ep'))
- route_gradient: float32 [32768, 8], P(('dp', 'ep'))
- gate_gradient: bfloat16 [7168, 8192], P('dp', 'ep')
- up_gradient: bfloat16 [7168, 8192], P('dp', 'ep')
- down_gradient: bfloat16 [7168, 8192], P('dp', 'ep')
Inputs may be any that keep to these rules, and one draw needn't show every extreme that they name: `expert_ids`: each row names 8 different ids, 2 in each of 4 groups of 32 consecutive ids. In each aligned block of 4096 rows, one id that is a multiple of 64 is named by 8 or more rows of every aligned block of 128 rows inside it.
All inputs are finite; a program needn't handle non-finite values.
Results may differ from a plain program's by a relative error of at most 0.014.
Values may be sent and summed in bfloat16 or wider, within the bound.
No kernel may reach another device: no remote copies, remote signals or barrier semaphores. Data moves between devices by JAX's collectives and lax.ppermute only.
A program may use at most 128 MiB of HBM per device.

v0:
```python
import math

import jax
import jax.numpy as jnp
from jax import lax
from jax.sharding import PartitionSpec as P

ROUTED = 256
TOPK = 8
SLICES = 8
CAP = 8


def in_one_piece(arrays, axis, split_dim, concat_dim, along):
    widths = [math.prod(a.shape[along:]) for a in arrays]
    both = jnp.concatenate(
        [a.reshape(*a.shape[:along], w) for a, w in zip(arrays, widths)], axis=along
    )
    filled = lax.all_to_all(both, axis, split_axis=split_dim, concat_axis=concat_dim, tiled=True)
    tiles = jnp.split(filled, [sum(widths[:k]) for k in range(1, len(widths))], axis=along)
    return tuple(
        (b.reshape(*filled.shape[:along], *a.shape[along:]) for a, b in zip(arrays, tiles))
    )


def hidden_terms(gate_pre, up_pre, projected, gate_rows):
    sigmoid = jax.nn.sigmoid(gate_pre)
    swished = gate_pre * sigmoid
    hidden = lax.optimization_barrier((swished * up_pre).astype(jnp.bfloat16)).astype(jnp.float32)
    route_part = jnp.sum(hidden * projected, axis=1).astype(jnp.bfloat16)
    scaling = gate_rows.astype(jnp.float32)[:, None]
    grad_hidden = scaling * projected
    gate_delta = grad_hidden * up_pre * sigmoid * (1.0 + gate_pre * (1.0 - sigmoid))
    up_delta = grad_hidden * swished
    deltas = jnp.concatenate([gate_delta, up_delta], axis=1).astype(jnp.bfloat16)
    scaled = (scaling * hidden).astype(jnp.bfloat16)
    return (deltas, scaled, route_part)


def body(tokens, out_grad, expert_ids, route_weights, gate_matrix, up_matrix, down_matrix):
    senders = lax.axis_size("ep")
    experts = senders // SLICES
    stride = ROUTED // experts
    tok_rows = tokens.shape[0]
    width = tokens.shape[1]
    hid_width = gate_matrix.shape[1]
    flat_ids = expert_ids.reshape(tok_rows * TOPK)
    window = flat_ids % stride == 0
    expert = jnp.where(window, flat_ids // stride, experts)
    column = jnp.arange(experts, dtype=jnp.int32)
    onehot = (expert[:, None] == column[None, :]).astype(jnp.int32)
    earlier = jnp.cumsum(onehot, axis=0) - onehot
    slot_index = jnp.sum(earlier * onehot, axis=1)
    kept_entry = window & (slot_index < CAP)
    places = jnp.arange(experts * CAP, dtype=jnp.int32)
    assign = kept_entry[:, None] & ((expert * CAP + slot_index)[:, None] == places[None, :])
    assign = assign.astype(jnp.float32).reshape(tok_rows, TOPK, experts * CAP)
    select = jnp.sum(assign, axis=1).astype(jnp.bfloat16)
    slot_in = jnp.einsum("ts,td->sd", select, tokens, preferred_element_type=jnp.float32).astype(
        jnp.bfloat16
    )
    slot_grad = jnp.einsum(
        "ts,td->sd", select, out_grad, preferred_element_type=jnp.float32
    ).astype(jnp.bfloat16)
    slot_gate = jnp.einsum("tks,tk->s", assign, route_weights.astype(jnp.float32)).astype(
        jnp.bfloat16
    )
    send_in = jnp.repeat(slot_in.reshape(experts, CAP, width), SLICES, axis=0)
    send_grad = jnp.repeat(slot_grad.reshape(experts, CAP, width), SLICES, axis=0)
    send_gate = jnp.repeat(slot_gate.reshape(experts, CAP), SLICES, axis=0)
    rows_in, rows_grad, rows_gate = in_one_piece((send_in, send_grad, send_gate), "ep", 0, 0, 2)
    total_rows = senders * CAP
    rows_in = rows_in.reshape(total_rows, width)
    rows_grad = rows_grad.reshape(total_rows, width)
    rows_gate = rows_gate.reshape(total_rows)
    stacked = jnp.concatenate([gate_matrix, up_matrix], axis=1)
    full_pair, full_down = (
        lax.all_gather(stacked, "dp", axis=0, tiled=True),
        lax.all_gather(down_matrix, "dp", axis=0, tiled=True),
    )
    gate_up = jnp.dot(rows_in, full_pair, preferred_element_type=jnp.float32)
    projected = jnp.dot(rows_grad, full_down, preferred_element_type=jnp.float32)
    deltas, scaled, route_part = hidden_terms(
        gate_up[:, :hid_width], gate_up[:, hid_width:], projected, rows_gate
    )
    partial_value = jnp.einsum(
        "rh,dh->rd", deltas, full_pair, preferred_element_type=jnp.float32
    ).astype(jnp.bfloat16)
    left = jnp.einsum("rd,rh->dh", rows_in, deltas, preferred_element_type=jnp.float32)
    right = jnp.einsum("rd,rh->dh", rows_grad, scaled, preferred_element_type=jnp.float32)
    summed = lax.psum_scatter(
        jnp.concatenate([left, right], axis=1).astype(jnp.bfloat16),
        "dp",
        scatter_dimension=0,
        tiled=True,
    ).astype(jnp.float32)
    back_in, back_route = in_one_piece(
        (partial_value.reshape(senders, CAP, width), route_part.reshape(senders, CAP)),
        "ep",
        0,
        0,
        2,
    )
    slot_sums = jnp.sum(
        back_in.reshape(experts, SLICES, CAP, width).astype(jnp.float32), axis=1
    ).reshape(experts * CAP, width)
    route_sums = jnp.sum(
        back_route.reshape(experts, SLICES, CAP).astype(jnp.float32), axis=1
    ).reshape(experts * CAP)
    input_gradient = jnp.dot(select.astype(jnp.float32), slot_sums).astype(jnp.bfloat16)
    route_gradient = jnp.einsum("tks,s->tk", assign, route_sums)
    gate_gradient = summed[:, :hid_width].astype(jnp.bfloat16)
    up_gradient = summed[:, hid_width : 2 * hid_width].astype(jnp.bfloat16)
    down_gradient = summed[:, 2 * hid_width :].astype(jnp.bfloat16)
    return (input_gradient, route_gradient, gate_gradient, up_gradient, down_gradient)


def solution(mesh):
    return jax.shard_map(
        body,
        mesh=mesh,
        in_specs=(
            P(("dp", "ep"), None),
            P(("dp", "ep"), None),
            P(("dp", "ep"), None),
            P(("dp", "ep"), None),
            P("dp", "ep"),
            P("dp", "ep"),
            P("dp", "ep"),
        ),
        out_specs=(
            P(("dp", "ep"), None),
            P(("dp", "ep"), None),
            P("dp", "ep"),
            P("dp", "ep"),
            P("dp", "ep"),
        ),
        check_vma=False,
    )
```

profile of v0, /device:TPU:2, one launch (start us, length us, event | category | flops | bytes accessed | tf_op | source)
XLA Modules:
  0.0 537.9 jit_solution(14116264508713704503)
XLA Ops:
  7.2 2.3 pad_maximum_fusion.3
  9.5 0.8 copy.124
  10.3 0.1 reshape.211
  10.4 0.1 reshape.210
  10.5 1.1 reduce-window.6
  11.7 0.2 slice_reduce_fusion
  11.9 0.2 reduce-window.9
  12.2 0.1 reduce_sum.48
  12.3 0.7 compare_and_fusion
  13.1 0.7 fusion.33
  13.7 0.8 fusion.5
  14.6 0.1 reshape.217
  14.7 0.1 copy.128
  14.8 0.1 reshape_reshape.2
  14.9 0.2 copy.129
  15.1 0.4 fusion.2
  15.5 1.9 fusion.1
  17.4 0.4 broadcast_in_dim.27
  17.8 0.4 broadcast_in_dim.26
  18.2 3.5 pad_maximum_fusion.1
  21.7 14.3 %all-to-all-start = ((bf16[32,8,14337]{2,1,0:T(8,128)(2,1)}), bf16[32,8,14337]{2,1,0:T(8,128)(2,1)}, u32[]{:S(2)}, u32[]{:S(2)}) async-start(bf16[32,8,14337]{2,1,0:T(8,128)(2,1)} %pad_maximum_fusion.1), calls=%async_computation | async-start | bytes 14811136 | tf_op jit(solution)/shard_map/all_to_all | solution.py:19
  36.1 0.7 all-gather.3.cloned.1.call-update
  36.8 0.2 reduce-scatter.4.cloned.1.call-start
  37.0 225.5 %all-to-all-done = bf16[32,8,14337]{2,1,0:T(8,128)(2,1)} async-done(((bf16[32,8,14337]{2,1,0:T(8,128)(2,1)}), bf16[32,8,14337]{2,1,0:T(8,128)(2,1)}, u32[]{:S(2)}, u32[]{:S(2)}) %all-to-all-start) | async-done | bytes 7340576 | tf_op jit(solution)/shard_map/all_to_all | solution.py:19
  262.5 0.9 convert_reduce_fusion.1
  263.4 0.1 reshape.223
  263.6 7.3 %fusion.4 = f32[256,512]{0,1:T(8,128)S(1)} fusion(bf16[7168,512]{1,0:T(8,128)(2,1)} %all-gather.5.cloned.1.call-done, bf16[32,8,14337]{2,1,0:T(8,128)(2,1)} %all-to-all-done), kind=kOutput, calls=%fused_computation.16 | convolution fusion | flops 1879048192 | bytes 11534336 | tf_op jit(solution)/shard_map/dot_general | solution.py:81
  270.8 22.5 %all-gather.3.cloned.1.call-done = bf16[7168,256]{1,0:T(8,128)(2,1)} async-done(((bf16[896,256]{1,0:T(8,128)(2,1)}), bf16[7168,256]{1,0:T(8,128)(2,1)}) %all-gather.3.cloned.1.call-update) | async-done | bytes 3670032 | tf_op jit(solution)/shard_map/all_gather | solution.py:79
  293.3 4.7 multiply_convert_fusion.2
  298.0 3.2 convolution_convert_fusion.1
  301.2 4.1 convolution_convert_fusion
  305.3 7.8 %pad_maximum_fusion = bf16[7168,768]{0,1:T(8,128)(2,1)} fusion(bf16[7168,256]{0,1:T(8,128)(2,1)S(1)} %convolution_convert_fusion.1, bf16[7168,512]{0,1:T(8,128)(2,1)S(1)} %convolution_convert_fusion), kind=kLoop, calls=%fused_computation | loop fusion | flops 22020096 | bytes 22020096 | tf_op jit(solution)/shard_map/concatenate | solution.py:92
  313.1 14.7 %copy.141 = bf16[7168,768]{1,0:T(8,128)(2,1)} copy(bf16[7168,768]{0,1:T(8,128)(2,1)} %pad_maximum_fusion) | data formatting | bytes 22020096
  327.9 0.2 convert_element_type.108
  328.2 5.2 fusion
  333.4 0.3 pad_maximum_fusion.2
  333.7 140.2 %all_to_all.10 = bf16[32,8,7169]{2,1,0:T(8,128)(2,1)S(1)} all-to-all(bf16[32,8,7169]{2,1,0:T(8,128)(2,1)S(1)} %pad_maximum_fusion.2), channel_id=1, replica_groups=mesh['dp'=8,'ep'=32] {'ep'}, dimensions={0} | all-to-all | bytes 7341056 | tf_op jit(solution)/shard_map/all_to_all | solution.py:19
  473.9 1.9 copy-done.2
  475.8 0.1 copy.143
  476.0 0.1 reshape.225
  476.0 0.1 reduce_sum.52
  476.1 0.1 copy.134
  476.2 0.1 reshape.228
  476.3 0.7 fusion.18
  477.1 2.6 convert_reduce_fusion
  479.7 1.9 convolution_convert_fusion.3
  481.6 47.4 %reduce-scatter.4.cloned.1.call-done = bf16[896,768]{1,0:T(8,128)(2,1)} async-done(((bf16[7168,768]{1,0:T(8,128)(2,1)}), bf16[896,768]{1,0:T(8,128)(2,1)}) %reduce-scatter.4.cloned.1.call-update) | async-done | bytes 1376272
  529.0 2.4 fusion.46
  (20 shorter events, 0.5 us)
Async XLA Ops:
  7.2 8.0 %copy-start = (bf16[128,7168]{1,0:T(8,128)(2,1)S(1)}, bf16[128,7168]{1,0:T(8,128)(2,1)}, u32[]{:S(2)}) copy-start(bf16[128,7168]{1,0:T(8,128)(2,1)} %param.8) | copy-start | bytes 5505028
  7.2 256.4 %all-gather.5.cloned.1.call-start = ((), (), s32[]{:S(2)}) async-start(), calls=%async_computation.4 | async-start | bytes 8257536 | tf_op jit(solution)/shard_map/all_gather | solution.py:78
  21.7 240.7 %all-to-all-start = ((bf16[32,8,14337]{2,1,0:T(8,128)(2,1)}), bf16[32,8,14337]{2,1,0:T(8,128)(2,1)}, u32[]{:S(2)}, u32[]{:S(2)}) async-start(bf16[32,8,14337]{2,1,0:T(8,128)(2,1)} %pad_maximum_fusion.1), calls=%async_computation | async-start | bytes 14811136 | tf_op jit(solution)/shard_map/all_to_all | solution.py:19
  36.0 257.2 %all-gather.3.cloned.1.call-start = ((), (), s32[]{:S(2)}) async-start(), calls=%async_computation.3 | async-start | bytes 4128768 | tf_op jit(solution)/shard_map/all_gather | solution.py:79
  36.8 492.2 %reduce-scatter.4.cloned.1.call-start = ((), (), s32[]{:S(2)}) async-start(), calls=%async_computation.5 | async-start | bytes 12386304
  333.4 198.0 %copy-start.1 = (bf16[128,7168]{1,0:T(8,128)(2,1)S(1)}, bf16[128,7168]{1,0:T(8,128)(2,1)}, u32[]{:S(2)}) copy-start(bf16[128,7168]{1,0:T(8,128)(2,1)} %param.8) | copy-start | bytes 5505028
  473.9 1.9 copy-start.2
Sparse Core Ops, SparseCore 0:
  10.4 200.9 all-gather.4
  213.2 80.0 all-gather.2
  328.0 200.9 reduce-scatter.3
where the time goes:
time: 539 us; the launch traced here: 538 us
  waiting for transfers between devices  296 us (55%)
  blocking collectives  140 us (26%)
  matrix products  30.2 us (6%)
  local copies, waits for them, and re-layouts  22.4 us (4%)
  other arithmetic  20.5 us (4%)
  starting transfers between devices  14.6 us (3%)
  between operations  13.9 us (3%)
    all_to_all x1, waiting for transfers between devices, in_one_piece(): lax.all_to_all(both, axis, split_axis=split_dim, concat_axis=concat_dim,...  225 us
    all_to_all x1, blocking collectives, in_one_piece(): lax.all_to_all(both, axis, split_axis=split_dim, concat_axis=concat_dim,...  140 us
    unnamed x4, waiting for transfers between devices  48.1 us
    all_gather x1, waiting for transfers between devices, body(): lax.all_gather(down_matrix, 'dp', axis=0, tiled=True)  22.5 us
    unnamed x9, local copies, waits for them, and re-layouts  17.6 us
    all_to_all x1, starting transfers between devices, in_one_piece(): lax.all_to_all(both, axis, split_axis=split_dim, concat_axis=concat_dim,...  14.3 us
  transfers between devices with their start and end apart: 4, of which 3 were waited for; matrix products, arithmetic and copies ran while one was open for 6% of the time, Pallas kernels for 0%

commit v1 on v0

v1 whole, which is shorter than its diff:
```python
import jax
import jax.numpy as jnp
from jax import lax
from jax.sharding import Mesh, PartitionSpec as P

ROUTED = 256
TOPK = 8
SLICES = 8
CAP = 8
PAIR = 2
LANES = 128

EVERY = ("dp", "x", "y", "zh")
ACROSS = ("dp", "x", "zh")


def routes(expert_ids, route_weights, experts):
    rows = expert_ids.shape[0]
    stride = ROUTED // experts
    flat_ids = expert_ids.reshape(rows * TOPK)
    window = flat_ids % stride == 0
    expert = jnp.where(window, flat_ids // stride, experts)
    column = jnp.arange(experts, dtype=jnp.int32)
    onehot = (expert[:, None] == column[None, :]).astype(jnp.int32)
    earlier = jnp.cumsum(onehot, axis=0) - onehot
    slot_index = jnp.sum(earlier * onehot, axis=1)
    kept_entry = window & (slot_index < CAP)
    places = jnp.arange(experts * CAP, dtype=jnp.int32)
    assign = kept_entry[:, None] & ((expert * CAP + slot_index)[:, None] == places[None, :])
    assign = assign.astype(jnp.float32).reshape(rows, TOPK, experts * CAP)
    select = jnp.sum(assign, axis=1)
    weights = route_weights.astype(jnp.float32)
    weighted = jnp.sum(assign * weights[:, :, None], axis=1)
    inverse = assign / weights[:, :, None]
    return select.astype(jnp.bfloat16), weighted.astype(jnp.bfloat16), inverse


def dispatch(choose, values, parts, experts):
    slots = jnp.einsum("ts,td->sd", choose, values, preferred_element_type=jnp.float32)
    slots = slots.astype(jnp.bfloat16).reshape(experts, CAP, parts, -1)
    slots = jnp.transpose(slots, (2, 0, 1, 3))[:, :, None]
    width = slots.shape[-1]
    send = jnp.broadcast_to(slots, (parts, experts, PAIR, CAP, width))
    send = send.reshape(parts * experts * PAIR, CAP, width)
    got = lax.all_to_all(send, ACROSS, split_axis=0, concat_axis=0, tiled=True)
    return lax.all_gather(got.reshape(-1, width), "y", axis=0, tiled=True)


def body(tokens, out_grad, expert_ids, route_weights, gate_matrix, up_matrix, down_matrix):
    parts = lax.axis_size("dp")
    experts = lax.axis_size("x")
    turns = lax.axis_size("y")
    width = gate_matrix.shape[0]
    hid = gate_matrix.shape[1]
    select, weighted, inverse = routes(expert_ids, route_weights, experts)
    rows_in = dispatch(select, tokens, parts, experts)
    rows_grad = dispatch(weighted, out_grad, parts, experts)
    total = rows_in.shape[0]
    pair = jnp.concatenate([gate_matrix, up_matrix], axis=1)
    first = jnp.dot(rows_in, pair, preferred_element_type=jnp.float32).astype(jnp.bfloat16)
    second = jnp.dot(rows_grad, down_matrix, preferred_element_type=jnp.float32).astype(
        jnp.bfloat16
    )
    gate_up = lax.psum_scatter(first, "dp", scatter_dimension=0, tiled=True)
    projected = lax.psum_scatter(second, "dp", scatter_dimension=0, tiled=True)
    gate_pre = gate_up[:, :hid].astype(jnp.float32)
    up_pre = gate_up[:, hid:].astype(jnp.float32)
    projected = projected.astype(jnp.float32)
    sigmoid = jax.nn.sigmoid(gate_pre)
    swished = gate_pre * sigmoid
    hidden = swished * up_pre
    route_part = jnp.sum(hidden * projected, axis=1)
    gate_delta = projected * up_pre * sigmoid * (1.0 + gate_pre * (1.0 - sigmoid))
    up_delta = projected * swished
    mine = jnp.concatenate([gate_delta, up_delta, hidden], axis=1).astype(jnp.bfloat16)
    every = lax.all_gather(mine, "dp", axis=0, tiled=True)
    deltas = every[:, : 2 * hid]
    hiddens = every[:, 2 * hid :]
    partial = jnp.einsum("rh,dh->rd", deltas, pair, preferred_element_type=jnp.float32)
    own = lax.axis_index("dp")
    spread = jnp.where(
        jnp.arange(parts, dtype=jnp.int32)[:, None] == own, route_part[None, :], 0.0
    ).reshape(total, 1)
    partial = jnp.concatenate(
        [partial.astype(jnp.bfloat16), jnp.broadcast_to(spread, (total, LANES)).astype(jnp.bfloat16)],
        axis=1,
    )
    summed = lax.psum_scatter(partial, "y", scatter_dimension=0, tiled=True)
    summed = summed.reshape(parts * experts * PAIR, CAP, width + LANES)
    back = lax.all_to_all(summed, ACROSS, split_axis=0, concat_axis=0, tiled=True)
    back = back.reshape(parts, experts, PAIR, CAP, width + LANES).astype(jnp.float32)
    back = jnp.sum(back, axis=2)
    slot_sums = jnp.transpose(back[..., :width], (1, 2, 0, 3)).reshape(
        experts * CAP, parts * width
    )
    route_sums = jnp.sum(back[..., width], axis=0).reshape(experts * CAP)
    input_gradient = jnp.dot(select.astype(jnp.float32), slot_sums).astype(jnp.bfloat16)
    route_gradient = jnp.einsum("tks,s->tk", inverse, route_sums)
    left = jnp.einsum("rd,rh->dh", rows_in, deltas, preferred_element_type=jnp.float32)
    left = left.astype(jnp.bfloat16)
    right = jnp.einsum("rd,rh->dh", rows_grad, hiddens, preferred_element_type=jnp.float32)
    right = right.astype(jnp.bfloat16)
    return (input_gradient, route_gradient, left[:, :hid], left[:, hid:], right)


def solution(mesh):
    parts, senders = mesh.devices.shape
    experts = senders // SLICES
    finer = Mesh(mesh.devices.reshape(parts, experts, SLICES // PAIR, PAIR), EVERY)
    rows = P(EVERY, None)
    tiles = P("dp", ("x", "y", "zh"))
    return jax.shard_map(
        body,
        mesh=finer,
        in_specs=(rows, rows, rows, rows, tiles, tiles, tiles),
        out_specs=(rows, rows, tiles, tiles, tiles),
        check_vma=False,
    )
```

time: 539 us -> 380 us (0.71)
  blocking collectives: 140 us -> 68.7 us
  waiting for transfers between devices: 296 us -> 237 us
  local copies, waits for them, and re-layouts: 22.4 us -> 7.86 us
  other arithmetic: 20.5 us -> 12 us
    all_to_all x1, waiting for transfers between devices: 225 us -> 13.7 us  [body(): lax.all_to_all(summed, ACROSS, split_axis=0, concat_axis=0, tiled=True)]
    reduce_scatter x0 -> x3, waiting for transfers between devices: none -> 126 us  [the longest x1 48.5 us: body(): summed = lax.psum_scatter(partial, 'y', scatter_dimension=0, tiled=True)]
    all_gather x2 -> x3, waiting for transfers between devices: 22.5 us -> 96.7 us  [the longest x2 52.9 us: dispatch(): return lax.all_gather(got.reshape(-1, width), 'y', axis=0, tiled=True)]
    all_to_all x1 -> x2, blocking collectives: 140 us -> 68.7 us  [dispatch(): got = lax.all_to_all(send, ACROSS, split_axis=0, concat_axis=0, tiled=True)]
    unnamed x4 -> x6, waiting for transfers between devices: 48.1 us -> 0.1 us
    unnamed x9 -> x20, local copies, waits for them, and re-layouts: 17.6 us -> 1.83 us
    concatenate x4 -> x2, other arithmetic: 13.9 us -> 3.23 us  [the longest x1 2.45 us: body(): jnp.concatenate([partial.astype(jnp.bfloat16), jnp.broadcast_to(spread, (...]
    dot_general x8 -> x6, matrix products: 24.2 us -> 19.6 us  [the longest x1 5.98 us: body(): jnp.dot(rows_in, pair, preferred_element_type=jnp.float32)]
  transfers between devices with their start and end apart: 4 -> 7, of which waited for: 3 -> 7; matrix products, arithmetic and copies ran while one was open for 6% -> 7% of each run, Pallas kernels for 0% -> 0%
where the time goes in v1:
time: 380 us; the launch traced here: 377 us
  waiting for transfers between devices  237 us (62%)
  blocking collectives  68.7 us (18%)
  matrix products  26.4 us (7%)
  between operations  14.4 us (4%)
  other arithmetic  12 us (3%)
  starting transfers between devices  10.8 us (3%)
  local copies, waits for them, and re-layouts  7.86 us (2%)
    all_to_all x2, blocking collectives, dispatch(): got = lax.all_to_all(send, ACROSS, split_axis=0, concat_axis=0, tiled=True)  68.7 us
    all_gather x2, waiting for transfers between devices, dispatch(): return lax.all_gather(got.reshape(-1, width), 'y', axis=0, tiled=True)  52.9 us
    reduce_scatter x1, waiting for transfers between devices, body(): summed = lax.psum_scatter(partial, 'y', scatter_dimension=0, tiled=True)  48.5 us
    all_gather x1, waiting for transfers between devices, body(): every = lax.all_gather(mine, 'dp', axis=0, tiled=True)  43.8 us
    reduce_scatter x1, waiting for transfers between devices, body(): gate_up = lax.psum_scatter(first, 'dp', scatter_dimension=0, tiled=True)  42.5 us
    reduce_scatter x1, waiting for transfers between devices, body(): projected = lax.psum_scatter(second, 'dp', scatter_dimension=0, tiled=True)  35.3 us
    all_to_all x1, waiting for transfers between devices, body(): lax.all_to_all(summed, ACROSS, split_axis=0, concat_axis=0, tiled=True)  13.7 us
    all_to_all x1, starting transfers between devices, body(): lax.all_to_all(summed, ACROSS, split_axis=0, concat_axis=0, tiled=True)  10.6 us
  transfers between devices with their start and end apart: 7, of which 7 were waited for; matrix products, arithmetic and copies ran while one was open for 7% of the time, Pallas kernels for 0%

profile of v1, /device:TPU:2, one launch (start us, length us, event | category | flops | bytes accessed | tf_op | source)
XLA Modules:
  0.0 376.9 jit_solution(15143891030813852870)
XLA Ops:
  7.2 0.9 copy.43
  8.1 0.1 reshape.206
  8.2 0.1 reshape.207
  8.4 1.1 reduce-window.6
  9.5 0.2 slice_reduce_fusion.1
  9.7 0.2 reduce-window.9
  9.9 0.1 add_bitcast_fusion
  10.0 0.1 reduce_sum.57
  10.2 0.1 fusion.22
  10.2 0.7 convert_element_type.87
  11.0 0.1 copy.50
  11.1 0.1 convert_reduce_fusion.1
  11.2 0.4 convolution_convert_fusion.2
  11.6 0.1 broadcast_in_dim.57
  11.7 36.8 %all_to_all.15 = bf16[64,8,896]{2,1,0:T(8,128)(2,1)} all-to-all(bf16[64,8,896]{2,1,0:T(8,128)(2,1)S(1)} %bitcast.62), channel_id=1, replica_groups=mesh['dp'=8,'x'=4,'y'=4,'zh'=2] {'dp','x','zh'}, dimensions={0} | all-to-all | bytes 1835008 | tf_op jit(solution)/shard_map/all_to_all | solution.py:45
  48.5 1.9 convolution_convert_fusion.1
  50.5 0.1 broadcast_in_dim.58
  50.6 31.9 %all_to_all.16 = bf16[64,8,896]{2,1,0:T(8,128)(2,1)} all-to-all(bf16[64,8,896]{2,1,0:T(8,128)(2,1)S(1)} %bitcast.63), channel_id=1, replica_groups=mesh['dp'=8,'x'=4,'y'=4,'zh'=2] {'dp','x','zh'}, dimensions={0} | all-to-all | bytes 1835008 | tf_op jit(solution)/shard_map/all_to_all | solution.py:45
  82.6 10.4 %all-gather.4.cloned.1.call-done = bf16[2048,896]{1,0:T(8,128)(2,1)} async-done(((bf16[512,896]{1,0:T(8,128)(2,1)}), bf16[2048,896]{1,0:T(8,128)(2,1)}) %all-gather.4.cloned.1.call-update) | async-done | bytes 3670032 | tf_op jit(solution)/shard_map/all_gather | solution.py:46
  93.0 4.3 %convolution_convert_fusion.5 = bf16[2048,256]{1,0:T(8,128)(2,1)} fusion(bf16[2048,896]{1,0:T(8,128)(2,1)} %all-gather.4.cloned.1.call-done, bf16[896,256]{1,0:T(8,128)(2,1)S(1)} %copy-done.7), kind=kOutput, calls=%fused_computation.6 | convolution fusion | flops 940048384 | bytes 5177344 | tf_op jit(solution)/shard_map/dot_general | solution.py:61
  97.3 0.8 constant_dynamic-update-slice_fusion.1
  98.1 0.8 constant_dynamic-update-slice_fusion
  99.0 42.6 %all-gather.6.cloned.1.call-done = bf16[2048,896]{1,0:T(8,128)(2,1)} async-done(((bf16[512,896]{1,0:T(8,128)(2,1)}), bf16[2048,896]{1,0:T(8,128)(2,1)}) %all-gather.6.cloned.1.call-update) | async-done | bytes 3670032 | tf_op jit(solution)/shard_map/all_gather | solution.py:46
  141.5 6.0 %convolution_convert_fusion.4 = bf16[2048,512]{1,0:T(8,128)(2,1)} fusion(bf16[2048,896]{1,0:T(8,128)(2,1)} %all-gather.6.cloned.1.call-done, bf16[896,512]{1,0:T(8,128)(2,1)} %constant_dynamic-update-slice_fusion), kind=kOutput, calls=%fused_computation.5 | convolution fusion | flops 1880096768 | bytes 6684672 | tf_op jit(solution)/shard_map/dot_general | solution.py:60
  147.6 35.3 %reduce-scatter.4.cloned.1.call-done = bf16[256,256]{1,0:T(8,128)(2,1)} async-done(((bf16[2048,256]{1,0:T(8,128)(2,1)}), bf16[256,256]{1,0:T(8,128)(2,1)}) %reduce-scatter.4.cloned.1.call-update) | async-done | bytes 131088 | tf_op jit(solution)/shard_map/reduce_scatter | solution.py:65
  182.9 42.5 %reduce-scatter.6.cloned.1.call-done = bf16[256,512]{1,0:T(8,128)(2,1)} async-done(((bf16[2048,512]{1,0:T(8,128)(2,1)}), bf16[256,512]{1,0:T(8,128)(2,1)}) %reduce-scatter.6.cloned.1.call-update) | async-done | bytes 262160 | tf_op jit(solution)/shard_map/reduce_scatter | solution.py:64
  225.4 1.3 fusion.10
  226.7 0.8 pad_maximum_fusion.1
  227.5 0.1 fusion.34
  227.6 43.8 %all-gather.8.cloned.1.call-done = bf16[2048,768]{1,0:T(8,128)(2,1)} async-done(((bf16[256,768]{1,0:T(8,128)(2,1)}), bf16[2048,768]{1,0:T(8,128)(2,1)}) %all-gather.8.cloned.1.call-update) | async-done | bytes 3145744 | tf_op jit(solution)/shard_map/all_gather | solution.py:76
  271.4 3.9 %convolution_convert_fusion.3 = bf16[2048,896]{0,1:T(8,128)(2,1)S(1)} fusion(bf16[896,512]{1,0:T(8,128)(2,1)} %constant_dynamic-update-slice_fusion, bf16[2048,768]{1,0:T(8,128)(2,1)} %all-gather.8.cloned.1.call-done), kind=kOutput, calls=%fused_computation.4 | convolution fusion | flops 1880883200 | bytes 6684672 | tf_op jit(solution)/shard_map/rh,dh->rd/dot_general | solution.py:79
  275.4 2.5 pad_maximum_fusion
  277.8 48.5 %reduce-scatter.8.cloned.1.call-done = bf16[512,1024]{0,1:T(8,128)(2,1)} async-done(((bf16[2048,1024]{0,1:T(8,128)(2,1)}), bf16[512,1024]{0,1:T(8,128)(2,1)}) %reduce-scatter.8.cloned.1.call-update) | async-done | bytes 1048592 | tf_op jit(solution)/shard_map/reduce_scatter | solution.py:88
  326.4 2.3 copy.53
  328.6 10.6 %all-to-all-start.2 = ((bf16[64,8,1024]{2,1,0:T(8,128)(2,1)}), bf16[64,8,1024]{2,1,0:T(8,128)(2,1)S(1)}, u32[]{:S(2)}, u32[]{:S(2)}) async-start(bf16[64,8,1024]{2,1,0:T(8,128)(2,1)} %bitcast.59), calls=%async_computation.5 | async-start | bytes 2097152 | tf_op jit(solution)/shard_map/all_to_all | solution.py:90
  339.2 0.1 copy.55
  339.3 4.6 %fusion.7 = f32[128,8,1,32]{3,2,1,0:T(1,128)S(1)} fusion(pred[128,8]{1,0:T(8,128)(4,1)S(1)} %compare_and_fusion, f32[128,8]{1,0:T(8,128)S(1)} %copy.55, s32[128,8]{1,0:T(8,128)S(1)} %fusion.22), kind=kLoop, calls=%fused_computation.17 | loop fusion | flops 131072 | bytes 140288 | tf_op jit(solution)/shard_map/div | solution.py:34
  343.9 4.9 %fusion.3 = bf16[896,512]{1,0:T(8,128)(2,1)S(1)} fusion(bf16[2048,896]{1,0:T(8,128)(2,1)} %all-gather.6.cloned.1.call-done, bf16[2048,768]{1,0:T(8,128)(2,1)} %all-gather.8.cloned.1.call-done), kind=kOutput, calls=%fused_computation.12 | convolution fusion | flops 1879506944 | bytes 6684672 | tf_op jit(solution)/shard_map/rd,rh->dh/dot_general | solution.py:99
  348.8 1.0 fusion.41
  349.8 3.2 convolution_convert_fusion.6
  353.0 13.7 %all-to-all-done.2 = bf16[64,8,1024]{2,1,0:T(8,128)(2,1)S(1)} async-done(((bf16[64,8,1024]{2,1,0:T(8,128)(2,1)}), bf16[64,8,1024]{2,1,0:T(8,128)(2,1)S(1)}, u32[]{:S(2)}, u32[]{:S(2)}) %all-to-all-start.2) | async-done | bytes 1048608 | tf_op jit(solution)/shard_map/all_to_all | solution.py:90
  366.6 0.2 convert_reduce_fusion
  366.8 0.1 slice_reduce_fusion
  367.0 0.1 reshape.217
  367.1 0.2 multiply_reduce_fusion
  367.3 0.7 copy.60
  368.0 0.1 copy.66
  368.2 1.9 fusion.42
  (41 shorter events, 0.8 us)
Async XLA Ops:
  7.2 4.0 %copy-start = (bf16[128,7168]{1,0:T(8,128)(2,1)S(1)}, bf16[128,7168]{1,0:T(8,128)(2,1)}, u32[]{:S(2)}) copy-start(bf16[128,7168]{1,0:T(8,128)(2,1)} %param.8) | copy-start | bytes 5505028
  7.2 85.8 %all-gather.4.cloned.1.call-start = ((), (), s32[]{:S(2)}) async-start(), calls=%async_computation.6 | async-start | bytes 4587520 | tf_op jit(solution)/shard_map/all_gather | solution.py:46
  11.1 37.4 %copy-start.3 = (bf16[128,32]{0,1:T(8,128)(2,1)}, bf16[128,32]{0,1:T(8,128)(2,1)S(1)}, u32[]{:S(2)}) copy-start(bf16[128,32]{0,1:T(8,128)(2,1)S(1)} %get-tuple-element.5) | copy-start | bytes 24580
  48.5 93.0 %all-gather.6.cloned.1.call-start = ((), (), s32[]{:S(2)}) async-start(), calls=%async_computation.8 | async-start | bytes 4587520 | tf_op jit(solution)/shard_map/all_gather | solution.py:46
  48.5 44.4 %copy-start.7 = (bf16[896,256]{1,0:T(8,128)(2,1)S(1)}, bf16[896,256]{1,0:T(8,128)(2,1)}, u32[]{:S(2)}) copy-start(bf16[896,256]{1,0:T(8,128)(2,1)} %param.13) | copy-start | bytes 1376260
  82.5 14.8 %copy-start.1 = (bf16[896,256]{1,0:T(8,128)(2,1)S(1)}, bf16[896,256]{1,0:T(8,128)(2,1)}, u32[]{:S(2)}) copy-start(bf16[896,256]{1,0:T(8,128)(2,1)} %param.11) | copy-start | bytes 1376260
  82.6 15.6 %copy-start.2 = (bf16[896,256]{1,0:T(8,128)(2,1)S(1)}, bf16[896,256]{1,0:T(8,128)(2,1)}, u32[]{:S(2)}) copy-start(bf16[896,256]{1,0:T(8,128)(2,1)} %param.12) | copy-start | bytes 1376260
  82.6 100.3 %reduce-scatter.4.cloned.1.call-start = ((), (), s32[]{:S(2)}) async-start(), calls=%async_computation.7 | async-start | bytes 1179648 | tf_op jit(solution)/shard_map/reduce_scatter | solution.py:65
  97.3 128.1 %reduce-scatter.6.cloned.1.call-start = ((), (), s32[]{:S(2)}) async-start(), calls=%async_computation.9 | async-start | bytes 2359296 | tf_op jit(solution)/shard_map/reduce_scatter | solution.py:64
  147.5 123.9 %all-gather.8.cloned.1.call-start = ((), (), s32[]{:S(2)}) async-start(), calls=%async_computation.10 | async-start | bytes 3538944 | tf_op jit(solution)/shard_map/all_gather | solution.py:76
  227.5 98.9 %reduce-scatter.8.cloned.1.call-start = ((), (), s32[]{:S(2)}) async-start(), calls=%async_computation.11 | async-start | bytes 5242880 | tf_op jit(solution)/shard_map/reduce_scatter | solution.py:88
  277.8 61.4 %copy-start.5 = (bf16[128,8]{0,1:T(8,128)(2,1)S(1)}, bf16[128,8]{0,1:T(8,128)(2,1)}, u32[]{:S(2)}) copy-start(bf16[128,8]{0,1:T(8,128)(2,1)} %param.10) | copy-start | bytes 6148
  328.6 38.0 %all-to-all-start.2 = ((bf16[64,8,1024]{2,1,0:T(8,128)(2,1)}), bf16[64,8,1024]{2,1,0:T(8,128)(2,1)S(1)}, u32[]{:S(2)}, u32[]{:S(2)}) async-start(bf16[64,8,1024]{2,1,0:T(8,128)(2,1)} %bitcast.59), calls=%async_computation.5 | async-start | bytes 2097152 | tf_op jit(solution)/shard_map/all_to_all | solution.py:90
  343.9 5.9 %copy-start.6 = (bf16[2048,896]{1,0:T(8,128)(2,1)S(1)}, bf16[2048,896]{1,0:T(8,128)(2,1)}, u32[]{:S(2)}) copy-start(bf16[2048,896]{1,0:T(8,128)(2,1)} %all-gather.4.cloned.1.call-done) | copy-start | bytes 11010052
  353.0 15.2 %copy-start.4 = (bf16[128,32]{0,1:T(8,128)(2,1)S(1)}, bf16[128,32]{0,1:T(8,128)(2,1)}, u32[]{:S(2)}) copy-start(bf16[128,32]{0,1:T(8,128)(2,1)} %copy-done.3) | copy-start | bytes 24580
Sparse Core Ops, SparseCore 0:
  48.6 44.3 all-gather.3
  94.8 46.6 all-gather.5
  144.6 38.2 reduce-scatter.3
  185.3 40.0 reduce-scatter.5
  227.6 43.7 all-gather.7
  278.0 48.3 reduce-scatter.7
